TPU v7x, 512 devices: a 8x2x16 block of a 8x8x16 slice. The times are simulated.
512 devices in a mesh: rep: 2 (over y), seq: 16 (over z), head: 8 (over x), sub: 2 (over core).
Axes of the slice: x: 8, y: 2, z: 16, core: 2. Of those that a mesh axis runs over, the one named last changes fastest.
The devices are a block of a 8x8x16 slice.
Arguments:
- tokens: bfloat16 [32, 4096], P(('rep', 'sub'), 'seq'), parts along dimension 0, may hold values from -260 to 260
- attn_gain: float32 [4096], P('seq'), may hold values from 0.1 to 1.9
- w_query: bfloat16 [4096, 4096], P('seq', 'head'), may hold values from -0.09375 to 0.09375
- key_projection_weight: bfloat16 [4096, 1024], P('seq', 'head'), may hold values from -0.375 to 0.375
- value_projection_weight: bfloat16 [4096, 1024], P('seq', 'head'), may hold values from -0.375 to 0.375
- w_attn_out: bfloat16 [4096, 4096], P('head', 'seq'), may hold values from -0.09375 to 0.09375
- cache_keys: bfloat16 [32, 8, 8192, 128], P(('rep', 'sub'), 'head', 'seq'), parts along dimension 0, may hold values from -2500 to 2500
- stored_value_cache: bfloat16 [32, 8, 8192, 128], P(('rep', 'sub'), 'head', 'seq'), parts along dimension 0, may hold values from -12 to 12
- lengths: int32 [32], P(('rep', 'sub')), parts along dimension 0, may hold values from 4096 to 8192
- positions: int32 [32], P(('rep', 'sub')), parts along dimension 0, may hold values from 0 to 8191
- mamba_gain: float32 [4096], replicated, may hold values from 0.1 to 1.9
- w_in: bfloat16 [2, 4096, 8192], P(None, None, ('seq', 'head')), may hold values from -0.09375 to 0.09375
- conv_weight: float32 [4, 8192], P(None, ('seq', 'head')), may hold values from -3 to 3
- conv_bias: float32 [8192], P(('seq', 'head')), may hold values from -0.5 to 0.5
- conv_state: float32 [32, 3, 8192], P(('rep', 'sub'), None, ('seq', 'head')), parts along dimension 0, may hold values from -6 to 6
- w_xproj: bfloat16 [8192, 288], P(('seq', 'head')), may hold values from -0.0625 to 0.0625
- w_dt: bfloat16 [256, 8192], P(None, ('seq', 'head')), may hold values from -0.375 to 0.375
- dt_bias: float32 [8192], P(('seq', 'head')), may hold values from -4 to 0
- a_log: float32 [16, 8192], P(None, ('seq', 'head')), may hold values from 0 to 2.77
- skip_gain: float32 [8192], P(('seq', 'head')), may hold values from 0.25 to 2
- ssm_state: float32 [32, 16, 8192], P(('rep', 'sub'), None, ('seq', 'head')), parts along dimension 0, may hold values from -6 to 6
- w_mamba_out: bfloat16 [8192, 4096], P(('seq', 'head')), may hold values from -0.25 to 0.25
Outputs:
- hidden_out: bfloat16 [32, 4096], P(('rep', 'sub'), 'seq'), parts along dimension 0
- new_state: float32 [32, 16, 8192], P(('rep', 'sub'), None, ('seq', 'head')), parts along dimension 0
There are 2 independent parts, one for each index of `rep`. A program takes and returns all parts, laid end to end along the dimension named above; an argument that names none is the same for every part. Nothing has to cross between parts.
Inputs may be any that keep to these rules, and one draw needn't show every extreme that they name: Cache positions p < lengths[b] hold sequence b's past keys and values; later positions are not attended.
All inputs are finite; a program needn't handle non-finite values.
Results may differ from a plain program's by a relative error of at most 0.015.
Values may be sent and summed in bfloat16 or wider, within the bound.
A program may use at most 64 MiB of HBM per device.

v0:
```python
import math
import jax
import jax.numpy as jnp
from jax import lax
from jax.sharding import PartitionSpec as P

norm_eps = 1e-05
masked_floor = -1e30
rope_base = 10000.0


def copy_for_each(value, axis):
    peers = lax.axis_size(axis)
    return lax.all_to_all(
        jnp.broadcast_to(value[None], (peers, *value.shape)), axis, 0, 0, tiled=True
    )


def taken_together(value, axis):
    everything = copy_for_each(value, axis)
    return jnp.sum(everything, axis=0)


def together(arrays, axis):
    line, at, done = (jnp.concatenate([a.reshape(-1) for a in arrays]), 0, [])
    subtotal = taken_together(line, axis)
    for a in arrays:
        done.append(subtotal[at : at + a.size].reshape(a.shape))
        at += a.size
    return tuple(done)


def gathered_once(value, axis):
    leaves = jax.tree.leaves(value)
    turns = sorted(range(len(leaves)), key=lambda k: -leaves[k].size)
    width = (1, *leaves[turns[0]].shape)[-1]
    lines = [
        jnp.pad(leaves[k].reshape(-1), (0, -leaves[k].size % width)).reshape(-1, width)
        for k in turns
    ]
    both, at, found = (copy_for_each(jnp.concatenate(lines), axis), 0, {})
    for k, line in zip(turns, lines):
        section = both[:, at : at + len(line)].reshape(len(both), -1)
        found[k] = section[:, : leaves[k].size].reshape(-1, *leaves[k].shape)
        at += len(line)
    numbers = iter(range(len(leaves)))
    return jax.tree.map(lambda _: found[next(numbers)], value)


def combined_pairwise(pieces, combine):
    while len(jax.tree.leaves(pieces)[0]) > 1:
        pieces = jax.vmap(combine)(
            *(jax.tree.map(lambda part: part[side::2], pieces) for side in (0, 1))
        )
    return jax.tree.map(lambda part: part[0], pieces)


def merged(value, axis, combine):
    pieces = gathered_once(value, axis)
    return combined_pairwise(pieces, combine)


def in_order(blocks, dim):
    blocks = jnp.moveaxis(blocks, 0, dim)
    dims = blocks.shape
    return blocks.reshape(*dims[:dim], dims[dim] * dims[dim + 1], *dims[dim + 2 :])


def collect(value, axis, dim):
    return in_order(copy_for_each(value, axis), dim)


def over_axes(value, axes):
    for axis in axes:
        value = lax.psum(value, axis)
    return value


def in_blocks(value, dim, peers):
    dims = value.shape
    blocks = value.reshape(*dims[:dim], peers, dims[dim] // peers, *dims[dim + 1 :])
    return jnp.moveaxis(blocks, dim, 0)


def sent_and_summed(value, axis, dim):
    peers = lax.axis_size(axis)
    blocks = lax.all_to_all(in_blocks(value, dim, peers), axis, 0, 0, tiled=True)
    return jnp.sum(blocks.astype(jnp.float32), axis=0)


def apply_rotary(vectors, positions):
    half_dim = vectors.shape[-1] // 2
    frequency = jnp.exp(
        -math.log(rope_base) * 2.0 * jnp.arange(half_dim, dtype=jnp.float32) / (2 * half_dim)
    )
    angles = positions.astype(jnp.float32)[:, None] * frequency[None, :]
    cosine = jnp.cos(angles)[:, None, :]
    sine_part = jnp.sin(angles)[:, None, :]
    first_half = vectors[..., :half_dim]
    second_half = vectors[..., half_dim:]
    return jnp.concatenate(
        [
            first_half * cosine - second_half * sine_part,
            second_half * cosine + first_half * sine_part,
        ],
        axis=-1,
    )


def join_partial(earlier, later):
    max_one, sum_one, acc_one = earlier
    max_two, sum_two, acc_two = later
    joined_max = jnp.maximum(max_one, max_two)
    factor_one = jnp.exp(max_one - joined_max)
    factor_two = jnp.exp(max_two - joined_max)
    return (
        joined_max,
        sum_one * factor_one + sum_two * factor_two,
        acc_one * factor_one[..., None] + acc_two * factor_two[..., None],
    )


def local(
    tokens,
    attn_gain,
    w_query,
    key_projection_weight,
    value_projection_weight,
    w_attn_out,
    cache_keys,
    stored_value_cache,
    lengths,
    positions,
    mamba_gain,
    w_in,
    conv_weight,
    conv_bias,
    conv_state,
    w_xproj,
    w_dt,
    dt_bias,
    a_log,
    skip_gain,
    ssm_state,
    w_mamba_out,
):
    batch_rows = tokens.shape[0]
    feature_cols = tokens.shape[1]
    head_dim = cache_keys.shape[3]
    kv_local = cache_keys.shape[1]
    ctx_local = cache_keys.shape[2]
    q_local = w_query.shape[1] // head_dim
    query_group_count = q_local // kv_local
    model_width = feature_cols * lax.axis_size("seq")
    token_float = tokens.astype(jnp.float32)
    lifted = (token_float * attn_gain[None, :]).astype(jnp.bfloat16)
    part_query = jnp.dot(lifted, w_query, preferred_element_type=jnp.float32)
    part_key = jnp.dot(lifted, key_projection_weight, preferred_element_type=jnp.float32)
    part_value = jnp.dot(lifted, value_projection_weight, preferred_element_type=jnp.float32)
    squares = jnp.sum(token_float * token_float, axis=1)
    part_query, part_key, part_value, sum_squares = together(
        (part_query, part_key, part_value, squares), "seq"
    )
    inv_rms = lax.rsqrt(sum_squares / model_width + norm_eps)
    query_vectors = apply_rotary(
        (part_query * inv_rms[:, None]).reshape(batch_rows, q_local, head_dim), positions
    ).astype(jnp.bfloat16)
    fresh_key_rows = apply_rotary(
        (part_key * inv_rms[:, None]).reshape(batch_rows, kv_local, head_dim), positions
    ).astype(jnp.bfloat16)
    fresh_value_rows = (
        (part_value * inv_rms[:, None]).reshape(batch_rows, kv_local, head_dim).astype(jnp.bfloat16)
    )
    grouped_queries = query_vectors.reshape(batch_rows, kv_local, query_group_count, head_dim)
    score_scale = head_dim ** (-0.5)
    scores = (
        jnp.einsum(
            "bhgd,bhtd->bhgt", grouped_queries, cache_keys, preferred_element_type=jnp.float32
        )
        * score_scale
    )
    slot_index = lax.axis_index("seq") * ctx_local + jnp.arange(ctx_local, dtype=jnp.int32)
    live_mask = slot_index[None, None, None, :] < lengths[:, None, None, None]
    local_max = jnp.max(jnp.where(live_mask, scores, masked_floor), axis=-1)
    weights = jnp.where(live_mask, jnp.exp(scores - local_max[..., None]), 0.0)
    local_sum = jnp.sum(weights, axis=-1)
    local_acc = jnp.einsum(
        "bhgt,bhtd->bhgd",
        weights.astype(jnp.bfloat16),
        stored_value_cache,
        preferred_element_type=jnp.float32,
    )
    merged_max, merged_sum, merged_acc = merged(
        (local_max, local_sum, local_acc), "seq", join_partial
    )
    score_new = (
        jnp.einsum(
            "bhgd,bhd->bhg", grouped_queries.astype(jnp.float32), fresh_key_rows.astype(jnp.float32)
        )
        * score_scale
    )
    row_max = jnp.maximum(merged_max, score_new)
    old_factor = jnp.exp(merged_max - row_max)
    new_weight = jnp.exp(score_new - row_max)
    total_weight = merged_sum * old_factor + new_weight
    attended = (
        merged_acc * old_factor[..., None]
        + new_weight[..., None] * fresh_value_rows.astype(jnp.float32)[:, :, None, :]
    )
    attn_rows = (
        (attended / total_weight[..., None])
        .reshape(batch_rows, q_local * head_dim)
        .astype(jnp.bfloat16)
    )
    out_part = jnp.dot(attn_rows, w_attn_out, preferred_element_type=jnp.float32)
    summed = taken_together(out_part, "head")
    mid_stream = (token_float + summed).astype(jnp.bfloat16)
    full_tokens = collect(mid_stream, "seq", 1)
    full_float = full_tokens.astype(jnp.float32)
    inv_rms_two = lax.rsqrt(jnp.mean(full_float * full_float, axis=1) + norm_eps)
    lifted_two = (full_float * inv_rms_two[:, None] * mamba_gain[None, :]).astype(jnp.bfloat16)
    inner = jnp.dot(lifted_two, w_in[0], preferred_element_type=jnp.float32)
    gate_branch = jnp.dot(lifted_two, w_in[1], preferred_element_type=jnp.float32)
    window = jnp.concatenate([conv_state, inner[:, None, :]], axis=1)
    mixed = jnp.sum(window * conv_weight[None, :, :], axis=1) + conv_bias[None, :]
    activated = jax.nn.silu(mixed)
    proj_part = jnp.dot(activated.astype(jnp.bfloat16), w_xproj, preferred_element_type=jnp.float32)
    projected = over_axes(proj_part, ("seq", "head"))
    rank_width = w_dt.shape[0]
    state_width = ssm_state.shape[1]
    dt_low = projected[:, :rank_width].astype(jnp.bfloat16)
    input_map = projected[:, rank_width : rank_width + state_width]
    output_map = projected[:, rank_width + state_width :]
    step_size = jax.nn.softplus(
        jnp.dot(dt_low, w_dt, preferred_element_type=jnp.float32) + dt_bias[None, :]
    )
    decay = jnp.exp(step_size[:, None, :] * (-jnp.exp(a_log))[None, :, :])
    new_state = decay * ssm_state + (step_size * activated)[:, None, :] * input_map[:, :, None]
    readout = jnp.sum(output_map[:, :, None] * new_state, axis=1) + skip_gain[None, :] * activated
    gated = (readout * jax.nn.silu(gate_branch)).astype(jnp.bfloat16)
    mamba_part = jnp.dot(gated, w_mamba_out, preferred_element_type=jnp.float32)
    share = sent_and_summed(mamba_part.astype(jnp.bfloat16), "seq", 1)
    share = taken_together(share, "head")
    hidden_out = (mid_stream.astype(jnp.float32) + share).astype(jnp.bfloat16)
    return (hidden_out, new_state)


def solution(mesh):
    in_specs = (
        P(("rep", "sub"), "seq"),
        P("seq"),
        P("seq", "head"),
        P("seq", "head"),
        P("seq", "head"),
        P("head", "seq"),
        P(("rep", "sub"), "head", "seq", None),
        P(("rep", "sub"), "head", "seq", None),
        P(("rep", "sub")),
        P(("rep", "sub")),
        P(),
        P(None, None, ("seq", "head")),
        P(None, ("seq", "head")),
        P(("seq", "head")),
        P(("rep", "sub"), None, ("seq", "head")),
        P(("seq", "head"), None),
        P(None, ("seq", "head")),
        P(("seq", "head")),
        P(None, ("seq", "head")),
        P(("seq", "head")),
        P(("rep", "sub"), None, ("seq", "head")),
        P(("seq", "head"), None),
    )
    out_specs = (P(("rep", "sub"), "seq"), P(("rep", "sub"), None, ("seq", "head")))
    return jax.shard_map(local, mesh=mesh, in_specs=in_specs, out_specs=out_specs, check_vma=False)
```

profile of v0, /device:TPU:80, one launch (start us, length us, event | category | flops | bytes accessed | tf_op | source)
XLA Modules:
  0.0 256.3 jit_solution(7575589292232890467)
XLA Ops:
  0.7 0.9 fusion.26
  1.6 1.1 convolution_bitcast_fusion
  2.8 0.1 convolution_bitcast_fusion.1
  2.9 0.7 copy-done.6
  3.6 0.1 convolution_bitcast_fusion.2
  3.7 1.0 broadcast_in_dim.31
  4.7 43.8 %all-to-all-start = ((f32[16,1,6152]{2,1,0:T(1,128)}), f32[16,1,6152]{2,1,0:T(1,128)S(1)}, u32[]{:S(2)}, u32[]{:S(2)}) async-start(f32[16,1,6152]{2,1,0:T(1,128)} %broadcast_in_dim.31), calls=%async_computation | async-start | bytes 802816 | tf_op jit(solution)/shard_map/all_to_all | solution.py:14
  48.8 23.8 %all-to-all-done = f32[16,1,6152]{2,1,0:T(1,128)S(1)} async-done(((f32[16,1,6152]{2,1,0:T(1,128)}), f32[16,1,6152]{2,1,0:T(1,128)S(1)}, u32[]{:S(2)}, u32[]{:S(2)}) %all-to-all-start) | async-done | bytes 393760 | tf_op jit(solution)/shard_map/all_to_all | solution.py:14
  72.6 0.3 reduce_sum.82
  73.0 0.5 select_reduce_fusion
  73.6 0.2 fusion.11
  73.9 0.3 fusion
  74.2 0.8 broadcast_in_dim.34
  75.0 6.1 %all-to-all-start.1 = ((f32[16,34,128]{2,1,0:T(8,128)}), f32[16,34,128]{2,1,0:T(8,128)S(1)}, u32[]{:S(2)}, u32[]{:S(2)}) async-start(f32[16,34,128]{2,1,0:T(8,128)} %broadcast_in_dim.34), calls=%async_computation.1 | async-start | bytes 655360 | tf_op jit(solution)/shard_map/all_to_all | solution.py:14
  81.4 0.2 fusion.51
  81.7 19.9 %all-to-all-done.1 = f32[16,34,128]{2,1,0:T(8,128)S(1)} async-done(((f32[16,34,128]{2,1,0:T(8,128)}), f32[16,34,128]{2,1,0:T(8,128)S(1)}, u32[]{:S(2)}, u32[]{:S(2)}) %all-to-all-start.1) | async-done | bytes 278560 | tf_op jit(solution)/shard_map/all_to_all | solution.py:14
  101.8 0.1 slice.142
  102.4 0.2 copy.147
  102.5 0.2 slice.138
  102.7 0.2 slice.143
  103.4 0.1 multiply_add_fusion
  103.6 0.2 slice.144
  103.8 0.2 slice.147
  104.3 0.1 multiply_add_fusion.2
  104.5 0.2 slice.148
  104.7 0.2 slice.151
  105.4 0.1 multiply_add_fusion.3
  105.5 0.2 fusion.22
  105.7 0.2 fusion.23
  105.9 15.5 %all_to_all.31 = f32[8,8,256]{2,1,0:T(8,128)S(1)} all-to-all(f32[8,8,256]{2,1,0:T(8,128)S(1)} %broadcast_in_dim.35), channel_id=1, replica_groups=mesh['rep'=2,'seq'=16,'head'=8,'sub'=2] {'head'}, dimensions={0} | all-to-all | bytes 131072 | tf_op jit(solution)/shard_map/all_to_all | solution.py:14
  121.4 0.6 broadcast_in_dim.36
  122.0 6.5 %all-to-all-start.3 = ((bf16[16,8,256]{2,1,0:T(8,128)(2,1)}), bf16[16,8,256]{2,1,0:T(8,128)(2,1)S(1)}, u32[]{:S(2)}, u32[]{:S(2)}) async-start(bf16[16,8,256]{2,1,0:T(8,128)(2,1)} %broadcast_in_dim.36), calls=%async_computation.3 | async-start | bytes 131072 | tf_op jit(solution)/shard_map/all_to_all | solution.py:14
  128.6 0.7 copy-done.13
  129.3 12.0 %all-to-all-done.3 = bf16[16,8,256]{2,1,0:T(8,128)(2,1)S(1)} async-done(((bf16[16,8,256]{2,1,0:T(8,128)(2,1)}), bf16[16,8,256]{2,1,0:T(8,128)(2,1)S(1)}, u32[]{:S(2)}, u32[]{:S(2)}) %all-to-all-start.3) | async-done | bytes 65568 | tf_op jit(solution)/shard_map/all_to_all | solution.py:14
  141.2 0.1 fusion.8
  141.5 0.2 convolution_bitcast_fusion.3
  141.8 0.5 copy-done.11
  142.4 0.5 copy-done.14
  142.9 0.1 fusion.64
  143.0 54.0 %psum.14 = f32[8,288]{1,0:T(8,128)S(1)} all-reduce(f32[8,288]{1,0:T(8,128)S(1)} %fusion.64), channel_id=1, replica_groups=mesh['rep'=2,'seq'=16,'head'=8,'sub'=2] {'seq'}, use_global_device_ids=true, to_apply=%region_7.8 | all-reduce | flops 2304 | bytes 18432 | tf_op jit(solution)/shard_map/psum | solution.py:75
  197.1 27.5 %psum.15 = f32[8,288]{1,0:T(8,128)S(1)} all-reduce(f32[8,288]{1,0:T(8,128)S(1)} %psum.14), channel_id=1, replica_groups=mesh['rep'=2,'seq'=16,'head'=8,'sub'=2] {'head'}, use_global_device_ids=true, to_apply=%region_8.9 | all-reduce | flops 2304 | bytes 18432 | tf_op jit(solution)/shard_map/psum | solution.py:75
  224.6 0.1 fusion.79
  224.8 0.7 multiply_reduce_fusion
  225.5 0.7 copy-done.17
  226.2 0.6 convolution_convert_fusion
  226.7 17.0 %all_to_all.32 = bf16[16,8,256]{2,1,0:T(8,128)(2,1)S(1)} all-to-all(bf16[16,8,256]{2,1,0:T(8,128)(2,1)S(1)} %bitcast.133), channel_id=1, replica_groups=mesh['rep'=2,'seq'=16,'head'=8,'sub'=2] {'seq'}, dimensions={0} | all-to-all | bytes 131072 | tf_op jit(solution)/shard_map/all_to_all | solution.py:87
  243.7 11.9 %all_to_all.33 = f32[8,8,256]{2,1,0:T(8,128)S(1)} all-to-all(f32[8,8,256]{2,1,0:T(8,128)S(1)} %broadcast_in_dim.38), channel_id=1, replica_groups=mesh['rep'=2,'seq'=16,'head'=8,'sub'=2] {'head'}, dimensions={0} | all-to-all | bytes 131072 | tf_op jit(solution)/shard_map/all_to_all | solution.py:14
  255.7 0.6 add_convert_fusion.1
  (99 shorter events, 3.2 us)
Async XLA Ops:
  0.6 72.4 %copy-start = (bf16[8,1,512,128]{3,2,1,0:T(8,128)(2,1)S(1)}, bf16[8,1,512,128]{3,2,1,0:T(8,128)(2,1)}, u32[]{:S(2)}) copy-start(bf16[8,1,512,128]{3,2,1,0:T(8,128)(2,1)} %param.28) | copy-start | bytes 3145732
  0.6 0.9 copy-start.4
  1.6 1.2 copy-start.5
  1.6 1.2 copy-start.12
  2.7 0.8 copy-start.6
  4.7 43.8 %copy-start.20 = (s32[8]{0:T(128)S(1)}, s32[8]{0:T(128)}, u32[]{:S(2)}) copy-start(s32[8]{0:T(128)} %param.31) | copy-start | bytes 100
  4.7 43.9 %copy-start.18 = (s32[8]{0:T(128)S(1)}, s32[8]{0:T(128)}, u32[]{:S(2)}) copy-start(s32[8]{0:T(128)} %param.30) | copy-start | bytes 100
  4.7 67.9 %all-to-all-start = ((f32[16,1,6152]{2,1,0:T(1,128)}), f32[16,1,6152]{2,1,0:T(1,128)S(1)}, u32[]{:S(2)}, u32[]{:S(2)}) async-start(f32[16,1,6152]{2,1,0:T(1,128)} %broadcast_in_dim.31), calls=%async_computation | async-start | bytes 802816 | tf_op jit(solution)/shard_map/all_to_all | solution.py:14
  48.5 25.4 %copy-start.1 = (bf16[8,1,512,128]{3,2,1,0:T(8,128)(2,1)S(1)}, bf16[8,1,512,128]{3,2,1,0:T(8,128)(2,1)}, u32[]{:S(2)}) copy-start(bf16[8,1,512,128]{3,2,1,0:T(8,128)(2,1)} %param.29) | copy-start | bytes 3145732
  75.0 26.6 %all-to-all-start.1 = ((f32[16,34,128]{2,1,0:T(8,128)}), f32[16,34,128]{2,1,0:T(8,128)S(1)}, u32[]{:S(2)}, u32[]{:S(2)}) async-start(f32[16,34,128]{2,1,0:T(8,128)} %broadcast_in_dim.34), calls=%async_computation.1 | async-start | bytes 655360 | tf_op jit(solution)/shard_map/all_to_all | solution.py:14
  103.6 2.1 copy-start.19
  103.8 37.7 %copy-start.2 = (bf16[2,4096,64]{1,2,0:T(8,128)(2,1)S(1)}, bf16[2,4096,64]{1,2,0:T(8,128)(2,1)}, u32[]{:S(2)}) copy-start(bf16[2,4096,64]{1,2,0:T(8,128)(2,1)} %param.33) | copy-start | bytes 3145732
  122.0 6.5 %copy-start.10 = (f32[4096]{0:T(1024)S(1)}, f32[4096]{0:T(1024)}, u32[]{:S(2)}) copy-start(f32[4096]{0:T(1024)} %param.32) | copy-start | bytes 49156
  122.0 19.2 %all-to-all-start.3 = ((bf16[16,8,256]{2,1,0:T(8,128)(2,1)}), bf16[16,8,256]{2,1,0:T(8,128)(2,1)S(1)}, u32[]{:S(2)}, u32[]{:S(2)}) async-start(bf16[16,8,256]{2,1,0:T(8,128)(2,1)} %broadcast_in_dim.36), calls=%async_computation.3 | async-start | bytes 131072 | tf_op jit(solution)/shard_map/all_to_all | solution.py:14
  128.6 0.7 copy-start.13
  141.4 84.1 %copy-start.3 = (bf16[64,4096]{1,0:T(8,128)(2,1)S(1)}, bf16[64,4096]{1,0:T(8,128)(2,1)}, u32[]{:S(2)}) copy-start(bf16[64,4096]{1,0:T(8,128)(2,1)} %param.43) | copy-start | bytes 1572868
  141.5 0.8 copy-start.11
  141.5 0.8 copy-start.15
  141.5 0.9 copy-start.8
  142.3 0.7 copy-start.14
  142.3 82.4 %copy-start.16 = (f32[64]{0:T(128)S(1)}, f32[64]{0:T(128)}, u32[]{:S(2)}) copy-start(f32[64]{0:T(128)} %param.39) | copy-start | bytes 772
  142.9 81.7 %copy-start.9 = (bf16[256,64]{0,1:T(8,128)(2,1)S(1)}, bf16[256,64]{0,1:T(8,128)(2,1)}, u32[]{:S(2)}) copy-start(bf16[256,64]{0,1:T(8,128)(2,1)} %param.38) | copy-start | bytes 98308
  143.0 81.7 %copy-start.7 = (f32[8,16,64]{2,1,0:T(8,128)S(1)}, f32[8,16,64]{2,1,0:T(8,128)}, u32[]{:S(2)}) copy-start(f32[8,16,64]{2,1,0:T(8,128)} %param.42) | copy-start | bytes 98308
  225.5 0.7 copy-start.17
where the time goes:
time: 257 us; the launch traced here: 256 us
  blocking collectives  126 us (49%)
  starting transfers between devices  56.5 us (22%)
  waiting for transfers between devices  55.7 us (22%)
  local copies, waits for them, and re-layouts  9.12 us (4%)
  other arithmetic  4.35 us (2%)
  matrix products  3.63 us (1%)
    psum x2, blocking collectives, over_axes(): value = lax.psum(value, axis)  81.5 us
    all_to_all x3, starting transfers between devices, copy_for_each(): lax.all_to_all(jnp.broadcast_to(value[None], (peers, *value.shape)), axis...  56.5 us
    all_to_all x3, waiting for transfers between devices, copy_for_each(): lax.all_to_all(jnp.broadcast_to(value[None], (peers, *value.shape)), axis...  55.7 us
    all_to_all x2, blocking collectives, copy_for_each(): lax.all_to_all(jnp.broadcast_to(value[None], (peers, *value.shape)), axis...  27.4 us
    all_to_all x1, blocking collectives, sent_and_summed(): lax.all_to_all(in_blocks(value, dim, peers), axis, 0, 0, tiled=True)  17 us
  transfers between devices with their start and end apart: 3, of which 3 were waited for; matrix products, arithmetic and copies ran while one was open for 0% of the time, Pallas kernels for 0%

commit v1 on v0

--- a/solution.py
+++ b/solution.py
@@ -72,7 +72,7 @@
 
 def over_axes(value, axes):
     for axis in axes:
-        value = lax.psum(value, axis)
+        value = lax.all_gather(value, axis_name=axis).sum(axis=0)
     return value
 
 

time: 257 us -> 228 us (0.89)
  blocking collectives: 126 us -> 96.3 us
    psum x2 -> x0, blocking collectives: 81.5 us -> none  [over_axes(): value = lax.psum(value, axis)]
    all_gather x0 -> x2, blocking collectives: none -> 53 us  [over_axes(): value = lax.all_gather(value, axis_name=axis).sum(axis=0)]
where the time goes in v1:
time: 228 us; the launch traced here: 227 us
  blocking collectives  96.3 us (42%)
  starting transfers between devices  56.5 us (25%)
  waiting for transfers between devices  55.7 us (24%)
  local copies, waits for them, and re-layouts  9.18 us (4%)
  other arithmetic  4.39 us (2%)
  matrix products  3.63 us (2%)
    all_to_all x3, starting transfers between devices, copy_for_each(): lax.all_to_all(jnp.broadcast_to(value[None], (peers, *value.shape)), axis...  56.5 us
    all_to_all x3, waiting for transfers between devices, copy_for_each(): lax.all_to_all(jnp.broadcast_to(value[None], (peers, *value.shape)), axis...  55.7 us
    all_gather x2, blocking collectives, over_axes(): value = lax.all_gather(value, axis_name=axis).sum(axis=0)  53 us
    all_to_all x2, blocking collectives, copy_for_each(): lax.all_to_all(jnp.broadcast_to(value[None], (peers, *value.shape)), axis...  26.4 us
    all_to_all x1, blocking collectives, sent_and_summed(): lax.all_to_all(in_blocks(value, dim, peers), axis, 0, 0, tiled=True)  16.8 us
  transfers between devices with their start and end apart: 3, of which 3 were waited for; matrix products, arithmetic and copies ran while one was open for 0% of the time, Pallas kernels for 0%

profile of v1, /device:TPU:80, one launch (start us, length us, event | category | flops | bytes accessed | tf_op | source)
XLA Modules:
  0.0 226.8 jit_solution(343592398294317679)
XLA Ops:
  0.7 0.9 fusion.26
  1.6 1.1 convolution_bitcast_fusion
  2.8 0.1 convolution_bitcast_fusion.1
  2.9 0.7 copy-done.6
  3.6 0.1 convolution_bitcast_fusion.2
  3.7 1.0 broadcast_in_dim.31
  4.7 43.8 %all-to-all-start = ((f32[16,1,6152]{2,1,0:T(1,128)}), f32[16,1,6152]{2,1,0:T(1,128)S(1)}, u32[]{:S(2)}, u32[]{:S(2)}) async-start(f32[16,1,6152]{2,1,0:T(1,128)} %broadcast_in_dim.31), calls=%async_computation | async-start | bytes 802816 | tf_op jit(solution)/shard_map/all_to_all | solution.py:14
  48.8 23.8 %all-to-all-done = f32[16,1,6152]{2,1,0:T(1,128)S(1)} async-done(((f32[16,1,6152]{2,1,0:T(1,128)}), f32[16,1,6152]{2,1,0:T(1,128)S(1)}, u32[]{:S(2)}, u32[]{:S(2)}) %all-to-all-start) | async-done | bytes 393760 | tf_op jit(solution)/shard_map/all_to_all | solution.py:14
  72.6 0.3 reduce_sum.100
  73.0 0.5 select_reduce_fusion
  73.6 0.2 fusion.11
  73.9 0.3 fusion
  74.2 0.8 broadcast_in_dim.34
  75.0 6.1 %all-to-all-start.1 = ((f32[16,34,128]{2,1,0:T(8,128)}), f32[16,34,128]{2,1,0:T(8,128)S(1)}, u32[]{:S(2)}, u32[]{:S(2)}) async-start(f32[16,34,128]{2,1,0:T(8,128)} %broadcast_in_dim.34), calls=%async_computation.1 | async-start | bytes 655360 | tf_op jit(solution)/shard_map/all_to_all | solution.py:14
  81.4 0.2 fusion.51
  81.7 19.9 %all-to-all-done.1 = f32[16,34,128]{2,1,0:T(8,128)S(1)} async-done(((f32[16,34,128]{2,1,0:T(8,128)}), f32[16,34,128]{2,1,0:T(8,128)S(1)}, u32[]{:S(2)}, u32[]{:S(2)}) %all-to-all-start.1) | async-done | bytes 278560 | tf_op jit(solution)/shard_map/all_to_all | solution.py:14
  101.8 0.1 slice.142
  102.4 0.2 copy.147
  102.5 0.2 slice.138
  102.7 0.2 slice.143
  103.4 0.1 multiply_add_fusion
  103.6 0.2 slice.144
  103.8 0.2 slice.147
  104.3 0.1 multiply_add_fusion.2
  104.5 0.2 slice.148
  104.7 0.2 slice.151
  105.4 0.1 multiply_add_fusion.3
  105.5 0.2 fusion.22
  105.7 0.2 fusion.23
  105.9 15.5 %all_to_all.31 = f32[8,8,256]{2,1,0:T(8,128)S(1)} all-to-all(f32[8,8,256]{2,1,0:T(8,128)S(1)} %broadcast_in_dim.35), channel_id=1, replica_groups=mesh['rep'=2,'seq'=16,'head'=8,'sub'=2] {'head'}, dimensions={0} | all-to-all | bytes 131072 | tf_op jit(solution)/shard_map/all_to_all | solution.py:14
  121.4 0.6 broadcast_in_dim.36
  122.0 6.5 %all-to-all-start.3 = ((bf16[16,8,256]{2,1,0:T(8,128)(2,1)}), bf16[16,8,256]{2,1,0:T(8,128)(2,1)S(1)}, u32[]{:S(2)}, u32[]{:S(2)}) async-start(bf16[16,8,256]{2,1,0:T(8,128)(2,1)} %broadcast_in_dim.36), calls=%async_computation.3 | async-start | bytes 131072 | tf_op jit(solution)/shard_map/all_to_all | solution.py:14
  128.6 0.7 copy-done.13
  129.3 12.0 %all-to-all-done.3 = bf16[16,8,256]{2,1,0:T(8,128)(2,1)S(1)} async-done(((bf16[16,8,256]{2,1,0:T(8,128)(2,1)}), bf16[16,8,256]{2,1,0:T(8,128)(2,1)S(1)}, u32[]{:S(2)}, u32[]{:S(2)}) %all-to-all-start.3) | async-done | bytes 65568 | tf_op jit(solution)/shard_map/all_to_all | solution.py:14
  141.2 0.1 fusion.8
  141.5 0.2 convolution_bitcast_fusion.3
  141.8 0.4 copy-done.11
  142.3 0.1 fusion.64
  142.5 28.4 %all-gather = f32[128,288]{1,0:T(8,128)S(1)} all-gather(f32[8,288]{1,0:T(8,128)S(1)} %fusion.64), channel_id=2, replica_groups=mesh['rep'=2,'seq'=16,'head'=8,'sub'=2] {'seq'}, dimensions={0}, use_global_device_ids=true | all-gather | bytes 156672 | tf_op jit(solution)/shard_map/all_gather | solution.py:75
  170.9 24.7 %all-gather.1 = f32[64,288]{1,0:T(8,128)S(1)} all-gather(f32[8,288]{1,0:T(8,128)S(1)} %bitcast_reduce_fusion), channel_id=3, replica_groups=mesh['rep'=2,'seq'=16,'head'=8,'sub'=2] {'head'}, dimensions={0}, use_global_device_ids=true | all-gather | bytes 82944 | tf_op jit(solution)/shard_map/all_gather | solution.py:75
  195.6 0.7 copy-done.9
  196.3 0.1 fusion.79
  196.4 0.7 multiply_reduce_fusion
  197.2 0.7 copy-done.17
  197.8 0.6 convolution_convert_fusion
  198.4 16.8 %all_to_all.32 = bf16[16,8,256]{2,1,0:T(8,128)(2,1)S(1)} all-to-all(bf16[16,8,256]{2,1,0:T(8,128)(2,1)S(1)} %bitcast.137), channel_id=1, replica_groups=mesh['rep'=2,'seq'=16,'head'=8,'sub'=2] {'seq'}, dimensions={0} | all-to-all | bytes 131072 | tf_op jit(solution)/shard_map/all_to_all | solution.py:87
  215.2 10.9 %all_to_all.33 = f32[8,8,256]{2,1,0:T(8,128)S(1)} all-to-all(f32[8,8,256]{2,1,0:T(8,128)S(1)} %broadcast_in_dim.38), channel_id=1, replica_groups=mesh['rep'=2,'seq'=16,'head'=8,'sub'=2] {'head'}, dimensions={0} | all-to-all | bytes 131072 | tf_op jit(solution)/shard_map/all_to_all | solution.py:14
  226.2 0.6 add_convert_fusion.1
  (101 shorter events, 3.3 us)
Async XLA Ops:
  0.6 72.4 %copy-start = (bf16[8,1,512,128]{3,2,1,0:T(8,128)(2,1)S(1)}, bf16[8,1,512,128]{3,2,1,0:T(8,128)(2,1)}, u32[]{:S(2)}) copy-start(bf16[8,1,512,128]{3,2,1,0:T(8,128)(2,1)} %param.28) | copy-start | bytes 3145732
  0.6 0.9 copy-start.4
  1.6 1.2 copy-start.5
  1.6 1.2 copy-start.12
  2.7 0.8 copy-start.6
  4.7 43.8 %copy-start.20 = (s32[8]{0:T(128)S(1)}, s32[8]{0:T(128)}, u32[]{:S(2)}) copy-start(s32[8]{0:T(128)} %param.31) | copy-start | bytes 100
  4.7 43.9 %copy-start.18 = (s32[8]{0:T(128)S(1)}, s32[8]{0:T(128)}, u32[]{:S(2)}) copy-start(s32[8]{0:T(128)} %param.30) | copy-start | bytes 100
  4.7 67.9 %all-to-all-start = ((f32[16,1,6152]{2,1,0:T(1,128)}), f32[16,1,6152]{2,1,0:T(1,128)S(1)}, u32[]{:S(2)}, u32[]{:S(2)}) async-start(f32[16,1,6152]{2,1,0:T(1,128)} %broadcast_in_dim.31), calls=%async_computation | async-start | bytes 802816 | tf_op jit(solution)/shard_map/all_to_all | solution.py:14
  48.5 25.4 %copy-start.1 = (bf16[8,1,512,128]{3,2,1,0:T(8,128)(2,1)S(1)}, bf16[8,1,512,128]{3,2,1,0:T(8,128)(2,1)}, u32[]{:S(2)}) copy-start(bf16[8,1,512,128]{3,2,1,0:T(8,128)(2,1)} %param.29) | copy-start | bytes 3145732
  75.0 26.6 %all-to-all-start.1 = ((f32[16,34,128]{2,1,0:T(8,128)}), f32[16,34,128]{2,1,0:T(8,128)S(1)}, u32[]{:S(2)}, u32[]{:S(2)}) async-start(f32[16,34,128]{2,1,0:T(8,128)} %broadcast_in_dim.34), calls=%async_computation.1 | async-start | bytes 655360 | tf_op jit(solution)/shard_map/all_to_all | solution.py:14
  103.6 2.1 copy-start.19
  103.8 37.7 %copy-start.2 = (bf16[2,4096,64]{1,2,0:T(8,128)(2,1)S(1)}, bf16[2,4096,64]{1,2,0:T(8,128)(2,1)}, u32[]{:S(2)}) copy-start(bf16[2,4096,64]{1,2,0:T(8,128)(2,1)} %param.33) | copy-start | bytes 3145732
  122.0 6.5 %copy-start.10 = (f32[4096]{0:T(1024)S(1)}, f32[4096]{0:T(1024)}, u32[]{:S(2)}) copy-start(f32[4096]{0:T(1024)} %param.32) | copy-start | bytes 49156
  122.0 19.2 %all-to-all-start.3 = ((bf16[16,8,256]{2,1,0:T(8,128)(2,1)}), bf16[16,8,256]{2,1,0:T(8,128)(2,1)S(1)}, u32[]{:S(2)}, u32[]{:S(2)}) async-start(bf16[16,8,256]{2,1,0:T(8,128)(2,1)} %broadcast_in_dim.36), calls=%async_computation.3 | async-start | bytes 131072 | tf_op jit(solution)/shard_map/all_to_all | solution.py:14
  128.6 0.7 copy-start.13
  141.5 0.7 copy-start.11
  141.5 0.7 copy-start.15
  141.5 0.8 copy-start.8
  141.5 0.8 copy-start.14
  142.2 55.0 %copy-start.3 = (bf16[64,4096]{1,0:T(8,128)(2,1)S(1)}, bf16[64,4096]{1,0:T(8,128)(2,1)}, u32[]{:S(2)}) copy-start(bf16[64,4096]{1,0:T(8,128)(2,1)} %param.43) | copy-start | bytes 1572868
  170.9 24.8 %copy-start.16 = (f32[64]{0:T(128)S(1)}, f32[64]{0:T(128)}, u32[]{:S(2)}) copy-start(f32[64]{0:T(128)} %param.39) | copy-start | bytes 772
  195.5 0.8 copy-start.9
  195.5 0.9 copy-start.7
  197.2 0.7 copy-start.17
